TPU v7x, 32 devices: a whole 2x2x4 slice. The times are simulated.
32 devices in a mesh: dp: 4 (over y, core), tensor: 8 (over z, x).
Axes of the slice: x: 2, y: 2, z: 4, core: 2. Of those that a mesh axis runs over, the one named last changes fastest.
Arguments:
- grads: bfloat16 [4, 2, 7168, 2048], P('dp', None, 'tensor'), may hold values from -6 to 6
- master: float32 [2, 7168, 2048], P(None, 'dp', 'tensor'), may hold values from -0.0625 to 0.0625
- moment1: float32 [2, 7168, 2048], P(None, 'dp', 'tensor'), may hold values from -3 to 3
- moment2: float32 [2, 7168, 2048], P(None, 'dp', 'tensor'), may hold values from 1 to 30
- tokens: bfloat16 [1024, 7168], P('dp'), may hold values from -6 to 6
- route: int32 [512], P('dp'), may hold values from 0 to 255, as said below
Outputs:
- new_master: float32 [2, 7168, 2048], P(None, 'dp', 'tensor')
- new_moment1: float32 [2, 7168, 2048], P(None, 'dp', 'tensor')
- new_moment2: float32 [2, 7168, 2048], P(None, 'dp', 'tensor')
- rollout: bfloat16 [2, 7168, 2048], P(None, None, 'tensor')
- hidden: bfloat16 [512, 2048], P('dp', 'tensor')
Inputs may be any that keep to these rules, and one draw needn't show every extreme that they name: route[i] indexes one of the 256 tokens of the data rank that holds routed row i; within one data rank's 128 routed rows no token appears twice.
All inputs are finite; a program needn't handle non-finite values.
Results may differ from a plain program's by a relative error of at most 0.019.
Values may be sent and summed in bfloat16 or wider, within the bound.
No kernel may reach another device: no remote copies, remote signals or barrier semaphores. Data moves between devices by JAX's collectives and lax.ppermute only.
A program may use at most 128 MiB of HBM per device.

v0:
```python
import jax
import jax.numpy as jnp
from jax import lax
from jax.sharding import PartitionSpec as P


def body(grads, master, moment1, moment2, tokens, route):
    tensor_count = lax.axis_size("tensor")
    rank_count = lax.axis_size("dp")
    grad_local = grads[0]
    rows_tensor = grad_local.shape[1]
    hidden_width = grad_local.shape[2]
    col_width = hidden_width // tensor_count
    slab = rows_tensor // rank_count
    summed = lax.psum_scatter(grad_local, "dp", scatter_dimension=1, tiled=True).astype(jnp.float32)
    pieces = summed.reshape(2, slab, tensor_count, col_width)
    spread = lax.all_to_all(
        pieces.astype(jnp.bfloat16), "tensor", split_axis=2, concat_axis=1, tiled=True
    ).astype(pieces.dtype)
    spread = spread.reshape(2, rank_count, tensor_count // rank_count, slab, col_width)
    owned = lax.all_to_all(
        spread.astype(jnp.bfloat16), "dp", split_axis=1, concat_axis=3, tiled=True
    ).astype(spread.dtype)
    grad_total = owned.reshape(2, rows_tensor * tensor_count // rank_count, col_width)
    new_moment1 = 0.9 * moment1 + 0.1 * grad_total
    new_moment2 = 0.95 * moment2 + 0.05 * grad_total * grad_total
    first_fix = 1.0 - 0.9**10
    second_fix = 1.0 - 0.95**10
    step_size = (
        new_moment1 / first_fix / (jnp.sqrt(new_moment2 / second_fix) + 1e-08) + 0.1 * master
    )
    new_master = master - 0.003 * step_size
    rollout_shard = new_master.astype(jnp.bfloat16)
    replicated = lax.all_gather(rollout_shard, "dp", axis=1, tiled=True)
    picked = jnp.take(tokens, route, axis=0)
    both = jnp.einsum("rd,kdh->rkh", picked, replicated, preferred_element_type=jnp.float32)
    hidden = (jax.nn.silu(both[:, 0, :]) * both[:, 1, :]).astype(jnp.bfloat16)
    return (new_master, new_moment1, new_moment2, replicated, hidden)


def solution(mesh):
    in_specs = (
        P("dp", None, "tensor", None),
        P(None, "dp", "tensor"),
        P(None, "dp", "tensor"),
        P(None, "dp", "tensor"),
        P("dp", None),
        P("dp"),
    )
    out_specs = (
        P(None, "dp", "tensor"),
        P(None, "dp", "tensor"),
        P(None, "dp", "tensor"),
        P(None, None, "tensor"),
        P("dp", "tensor"),
    )
    return jax.shard_map(body, mesh=mesh, in_specs=in_specs, out_specs=out_specs, check_vma=False)
```

profile of v0, /device:TPU:0, one launch (start us, length us, event | category | flops | bytes accessed | tf_op | source)
XLA Modules:
  0.0 229.7 jit_solution(10080741824321627601)
XLA Ops:
  7.2 0.0 reduce-scatter.2.cloned.1.call-start
  7.2 0.7 reduce-scatter.2.cloned.1.call-update
  7.9 0.0 all-gather.2.cloned.1.call-start
  7.9 71.3 %reduce-scatter.2.cloned.1.call-done = bf16[2,224,2048]{2,1,0:T(8,128)(2,1)} async-done(((bf16[2,896,2048]{2,1,0:T(8,128)(2,1)}), bf16[2,224,2048]{2,1,0:T(8,128)(2,1)}) %reduce-scatter.2.cloned.1.call-update) | async-done | bytes 1835024 | tf_op jit(solution)/shard_map/reduce_scatter | solution.py:15
  79.2 1.7 copy.21
  80.9 47.8 %all_to_all.27 = bf16[2,224,8,256]{3,1,0,2:T(8,128)(2,1)S(1)} all-to-all(bf16[2,224,8,256]{3,1,0,2:T(8,128)(2,1)S(1)} %bitcast.31), channel_id=1, replica_groups=mesh['dp'=4,'tensor'=8] {'tensor'}, dimensions={2} | all-to-all | bytes 3670016 | tf_op jit(solution)/shard_map/all_to_all | solution.py:17
  128.7 0.1 copy.16
  128.8 25.3 %all_to_all.28 = bf16[2,4,2,224,256]{4,3,2,0,1:T(8,128)(2,1)S(1)} all-to-all(bf16[2,4,2,224,256]{4,3,2,0,1:T(8,128)(2,1)S(1)} %copy.16), channel_id=1, replica_groups=mesh['dp'=4,'tensor'=8] {'dp'}, dimensions={1} | all-to-all | bytes 3670016 | tf_op jit(solution)/shard_map/all_to_all | solution.py:21
  154.1 0.0 copy-start.3
  154.1 0.4 convert_bitcast_fusion
  154.5 0.0 copy-start.1
  154.5 0.0 copy-start.2
  154.5 0.4 copy.17
  154.9 1.2 copy-done.3
  156.1 1.2 copy-done.1
  157.4 1.0 copy-done.2
  158.4 0.0 copy-start.4
  158.4 5.7 %fusion.9 = (bf16[2,1792,256]{2,1,0:T(8,128)(2,1)}, f32[2,1792,256]{2,1,0:T(8,128)}, f32[2,1792,256]{2,1,0:T(8,128)}, f32[2,1792,256]{2,1,0:T(8,128)}) fusion(f32[2,1792,256]{2,1,0:T(8,128)S(1)} %copy-done.1, f32[2,1792,256]{2,1,0:T(8,128)S(1)} %bitcast.29, f32[2,1792,256]{2,1,0:T(8,128)S(1)} %copy-done.2, f32[2,1792,256]{2,1,0:T(8,128)S(1)} %copy-done.3), kind=kLoop, calls=%fused_computation.20 | loop fusion | flops 14680064 | bytes 27525120 | tf_op jit(solution)/shard_map/convert_element_type | solution.py:33
  164.1 0.0 all-gather.2.cloned.1.call-update
  164.1 0.0 copy-done.4
  164.1 5.9 %gather_fusion = bf16[128,7168]{1,0:T(8,128)(2,1)S(1)} fusion(bf16[256,7168]{1,0:T(8,128)(2,1)} %param.10, s32[1024]{0:T(1024)S(1)} %pad_clamp_fusion), kind=kCustom, calls=%fused_computation | custom fusion | bytes 3670528 | tf_op jit(solution)/shard_map/jit(_take)/gather | solution.py:35
  170.0 44.6 %all-gather.2.cloned.1.call-done = bf16[2,7168,256]{2,1,0:T(8,128)(2,1)} async-done(((bf16[2,1792,256]{2,1,0:T(8,128)(2,1)}), bf16[2,7168,256]{2,1,0:T(8,128)(2,1)}) %all-gather.2.cloned.1.call-update) | async-done | bytes 7340048 | tf_op jit(solution)/shard_map/all_gather | solution.py:34
  214.6 0.0 copy-start
  214.7 4.4 %fusion.1 = f32[128,2,256]{2,0,1:T(8,128)S(1)} fusion(bf16[2,7168,256]{2,1,0:T(8,128)(2,1)} %all-gather.2.cloned.1.call-done, bf16[128,7168]{1,0:T(8,128)(2,1)S(1)} %gather_fusion, pred[128]{0:T(512)(128)(4,1)S(1)} %compare_and_fusion), kind=kOutput, calls=%fused_computation.7 | convolution fusion | flops 940441600 | bytes 9437312 | tf_op jit(solution)/shard_map/rd,kdh->rkh/dot_general | solution.py:36
  219.0 0.7 fusion.7
  219.7 0.1 copy-done
  219.8 3.0 %copy.23 = bf16[2,7168,256]{2,1,0:T(8,128)(2,1)} copy(bf16[2,7168,256]{2,1,0:T(8,128)(2,1)S(1)} %copy-done) | data formatting | bytes 14680064
  (3 shorter events, 0.0 us)
Async XLA Ops:
  7.2 72.0 %reduce-scatter.2.cloned.1.call-start = ((), (), s32[]{:S(2)}) async-start(), calls=%async_computation.3 | async-start | bytes 9175040 | tf_op jit(solution)/shard_map/reduce_scatter | solution.py:15
  7.9 206.7 %all-gather.2.cloned.1.call-start = ((), (), s32[]{:S(2)}) async-start(), calls=%async_computation.4 | async-start | bytes 9175040 | tf_op jit(solution)/shard_map/all_gather | solution.py:34
  154.1 2.0 copy-start.3
  154.5 2.9 %copy-start.1 = (f32[2,1792,256]{2,1,0:T(8,128)S(1)}, f32[2,1792,256]{2,1,0:T(8,128)}, u32[]{:S(2)}) copy-start(f32[2,1792,256]{2,1,0:T(8,128)} %param.7) | copy-start | bytes 11010052
  154.5 3.9 %copy-start.2 = (f32[2,1792,256]{2,1,0:T(8,128)S(1)}, f32[2,1792,256]{2,1,0:T(8,128)}, u32[]{:S(2)}) copy-start(f32[2,1792,256]{2,1,0:T(8,128)} %param.8) | copy-start | bytes 11010052
  158.4 5.7 %copy-start.4 = (s32[128]{0:T(128)S(1)}, s32[128]{0:T(128)}, u32[]{:S(2)}) copy-start(s32[128]{0:T(128)} %param.11) | copy-start | bytes 1540
  214.6 5.2 %copy-start = (bf16[2,7168,256]{2,1,0:T(8,128)(2,1)S(1)}, bf16[2,7168,256]{2,1,0:T(8,128)(2,1)}, u32[]{:S(2)}) copy-start(bf16[2,7168,256]{2,1,0:T(8,128)(2,1)} %all-gather.2.cloned.1.call-done) | copy-start | bytes 22020100
Sparse Core Ops, SparseCore 0:
  10.5 68.6 reduce-scatter.1
  164.2 50.3 all-gather.1
where the time goes:
time: 230 us
  waiting for transfers between devices  117 us (51%)
  blocking collectives  73.1 us (32%)
  local copies, waits for them, and re-layouts  14.7 us (6%)
  between operations  14.1 us (6%)
  other arithmetic  6.75 us (3%)
  matrix products  4.38 us (2%)
    reduce_scatter x1, waiting for transfers between devices, body(): lax.psum_scatter(grad_local, 'dp', scatter_dimension=1, tiled=True)  71.3 us
    all_to_all x1, blocking collectives, body(): lax.all_to_all(pieces.astype(jnp.bfloat16), 'tensor', split_axis=2, conca...  47.8 us
    all_gather x1, waiting for transfers between devices, body(): replicated = lax.all_gather(rollout_shard, 'dp', axis=1, tiled=True)  44.6 us
    all_to_all x1, blocking collectives, body(): lax.all_to_all(spread.astype(jnp.bfloat16), 'dp', split_axis=1, concat_ax...  25.3 us
    unnamed x11, local copies, waits for them, and re-layouts  6.67 us
    gather x1, local copies, waits for them, and re-layouts, body(): picked = jnp.take(tokens, route, axis=0)  5.88 us
    convert_element_type x1, other arithmetic, body(): rollout_shard = new_master.astype(jnp.bfloat16)  5.66 us
  transfers between devices with their start and end apart: 2, of which 2 were waited for; matrix products, arithmetic and copies ran while one was open for 3% of the time, Pallas kernels for 0%

commit v1 on v0

--- a/solution.py
+++ b/solution.py
@@ -31,7 +31,13 @@
     )
     new_master = master - 0.003 * step_size
     rollout_shard = new_master.astype(jnp.bfloat16)
-    replicated = lax.all_gather(rollout_shard, "dp", axis=1, tiled=True)
+    n_dev = lax.axis_size("dp")
+    current, parts = (rollout_shard, [rollout_shard])
+    for _ in range(n_dev - 1):
+        current = lax.ppermute(current, "dp", [(i, (i + 1) % n_dev) for i in range(n_dev)])
+        parts.insert(0, current)
+    line = jnp.concatenate(parts, axis=1)
+    replicated = jnp.roll(line, (lax.axis_index("dp") + 1) * rollout_shard.shape[1], axis=1)
     picked = jnp.take(tokens, route, axis=0)
     both = jnp.einsum("rd,kdh->rkh", picked, replicated, preferred_element_type=jnp.float32)
     hidden = (jax.nn.silu(both[:, 0, :]) * both[:, 1, :]).astype(jnp.bfloat16)

time: 230 us -> 266 us (1.16)
  local copies, waits for them, and re-layouts: 14.7 us -> 37.9 us
  waiting for transfers between devices: 117 us -> 133 us
  matrix products: 4.38 us -> 1.16 us
    ppermute x0 -> x3, waiting for transfers between devices: none -> 61.2 us  [body(): lax.ppermute(current, 'dp', [(i, (i + 1) % n_dev) for i in range(n_dev)])]
    all_gather x1 -> x0, waiting for transfers between devices: 44.6 us -> none  [body(): replicated = lax.all_gather(rollout_shard, 'dp', axis=1, tiled=True)]
    unnamed x11 -> x23, local copies, waits for them, and re-layouts: 6.67 us -> 22.2 us
    dynamic_slice x0 -> x1, local copies, waits for them, and re-layouts: none -> 4.98 us  [body(): jnp.roll(line, (lax.axis_index('dp') + 1) * rollout_shard.shape[1], axis=1)]
    dot_general x1, matrix products: 4.38 us -> 1.16 us  [body(): jnp.einsum('rd,kdh->rkh', picked, replicated, preferred_element_type=jnp....]
  transfers between devices with their start and end apart: 2 -> 4, of which waited for: 2 -> 4; matrix products, arithmetic and copies ran while one was open for 3% -> 3% of each run, Pallas kernels for 0% -> 0%
where the time goes in v1:
time: 266 us
  waiting for transfers between devices  133 us (50%)
  blocking collectives  73.1 us (27%)
  local copies, waits for them, and re-layouts  37.9 us (14%)
  between operations  14.1 us (5%)
  other arithmetic  6.16 us (2%)
    reduce_scatter x1, waiting for transfers between devices, body(): lax.psum_scatter(grad_local, 'dp', scatter_dimension=1, tiled=True)  71.3 us
    ppermute x3, waiting for transfers between devices, body(): lax.ppermute(current, 'dp', [(i, (i + 1) % n_dev) for i in range(n_dev)])  61.2 us
    all_to_all x1, blocking collectives, body(): lax.all_to_all(pieces.astype(jnp.bfloat16), 'tensor', split_axis=2, conca...  47.8 us
    all_to_all x1, blocking collectives, body(): lax.all_to_all(spread.astype(jnp.bfloat16), 'dp', split_axis=1, concat_ax...  25.3 us
    unnamed x23, local copies, waits for them, and re-layouts  22.2 us
    gather x1, local copies, waits for them, and re-layouts, body(): picked = jnp.take(tokens, route, axis=0)  7.15 us
  transfers between devices with their start and end apart: 4, of which 4 were waited for; matrix products, arithmetic and copies ran while one was open for 3% of the time, Pallas kernels for 0%

profile of v1, /device:TPU:0, one launch (start us, length us, event | category | flops | bytes accessed | tf_op | source)
XLA Modules:
  0.0 265.6 jit_solution(1653928580319128521)
XLA Ops:
  7.2 0.0 reduce-scatter.2.cloned.1.call-start
  7.2 0.7 reduce-scatter.2.cloned.1.call-update
  7.9 71.3 %reduce-scatter.2.cloned.1.call-done = bf16[2,224,2048]{2,1,0:T(8,128)(2,1)} async-done(((bf16[2,896,2048]{2,1,0:T(8,128)(2,1)}), bf16[2,224,2048]{2,1,0:T(8,128)(2,1)}) %reduce-scatter.2.cloned.1.call-update) | async-done | bytes 1835024 | tf_op jit(solution)/shard_map/reduce_scatter | solution.py:15
  79.2 1.7 copy.21
  80.9 47.8 %all_to_all.27 = bf16[2,224,8,256]{3,1,0,2:T(8,128)(2,1)S(1)} all-to-all(bf16[2,224,8,256]{3,1,0,2:T(8,128)(2,1)S(1)} %bitcast.31), channel_id=1, replica_groups=mesh['dp'=4,'tensor'=8] {'tensor'}, dimensions={2} | all-to-all | bytes 3670016 | tf_op jit(solution)/shard_map/all_to_all | solution.py:17
  128.7 0.1 copy.16
  128.8 25.3 %all_to_all.28 = bf16[2,4,2,224,256]{4,3,2,0,1:T(8,128)(2,1)S(1)} all-to-all(bf16[2,4,2,224,256]{4,3,2,0,1:T(8,128)(2,1)S(1)} %copy.16), channel_id=1, replica_groups=mesh['dp'=4,'tensor'=8] {'dp'}, dimensions={1} | all-to-all | bytes 3670016 | tf_op jit(solution)/shard_map/all_to_all | solution.py:21
  154.1 0.0 copy-start.5
  154.1 0.4 convert_bitcast_fusion
  154.5 0.0 copy-start.3
  154.5 0.0 copy-start.4
  154.5 0.4 copy.17
  154.9 1.2 copy-done.5
  156.1 1.2 copy-done.3
  157.4 1.0 copy-done.4
  158.4 0.0 copy-start.7
  158.4 5.1 %fusion.9 = (bf16[2,1792,256]{2,1,0:T(8,128)(2,1)S(1)}, f32[2,1792,256]{2,1,0:T(8,128)}, f32[2,1792,256]{2,1,0:T(8,128)}, f32[2,1792,256]{2,1,0:T(8,128)}) fusion(f32[2,1792,256]{2,1,0:T(8,128)S(1)} %copy-done.3, f32[2,1792,256]{2,1,0:T(8,128)S(1)} %bitcast.29, f32[2,1792,256]{2,1,0:T(8,128)S(1)} %copy-done.4, f32[2,1792,256]{2,1,0:T(8,128)S(1)} %copy-done.5), kind=kLoop, calls=%fused_computation.29 | loop fusion | flops 14680064 | bytes 27525120 | tf_op jit(solution)/shard_map/convert_element_type | solution.py:33
  163.5 0.0 collective-permute-start
  163.5 22.6 %collective-permute-done = bf16[2,1792,256]{2,1,0:T(8,128)(2,1)S(1)} collective-permute-done((bf16[2,1792,256]{2,1,0:T(8,128)(2,1)S(1)}, bf16[2,1792,256]{2,1,0:T(8,128)(2,1)S(1)}, u32[]{:S(2)}, u32[]{:S(2)}) %collective-permute-start) | collective-permute-done | bytes 1835040 | tf_op jit(solution)/shard_map/ppermute | solution.py:37
  186.1 0.0 copy-start.1
  186.1 1.2 copy-done.1
  187.4 0.0 collective-permute-start.1
  187.4 22.8 %collective-permute-done.1 = bf16[2,1792,256]{2,1,0:T(8,128)(2,1)} collective-permute-done((bf16[2,1792,256]{2,1,0:T(8,128)(2,1)S(1)}, bf16[2,1792,256]{2,1,0:T(8,128)(2,1)}, u32[]{:S(2)}, u32[]{:S(2)}) %collective-permute-start.1) | collective-permute-done | bytes 1835040 | tf_op jit(solution)/shard_map/ppermute | solution.py:37
  210.1 0.0 collective-permute-start.2
  210.1 0.0 copy-done.7
  210.2 7.1 %gather_fusion = bf16[128,7168]{1,0:T(8,128)(2,1)} fusion(bf16[256,7168]{1,0:T(8,128)(2,1)} %param.10, s32[1024]{0:T(1024)S(1)} %pad_clamp_fusion), kind=kCustom, calls=%fused_computation | custom fusion | bytes 3670528 | tf_op jit(solution)/shard_map/jit(_take)/gather | solution.py:41
  217.3 0.0 copy-start.2
  217.3 15.8 %collective-permute-done.2 = bf16[2,1792,256]{2,1,0:T(8,128)(2,1)} collective-permute-done((bf16[2,1792,256]{2,1,0:T(8,128)(2,1)}, bf16[2,1792,256]{2,1,0:T(8,128)(2,1)}, u32[]{:S(2)}, u32[]{:S(2)}) %collective-permute-start.2) | collective-permute-done | bytes 1835040 | tf_op jit(solution)/shard_map/ppermute | solution.py:37
  233.1 2.9 %constant_dynamic-update-slice_fusion.7 = bf16[2,14336,256]{2,1,0:T(8,128)(2,1)} fusion(bf16[2,1792,256]{2,1,0:T(8,128)(2,1)} %collective-permute-done.2), kind=kLoop, calls=%fused_computation.23 | loop fusion | bytes 3670016
  236.0 2.9 %constant_dynamic-update-slice_fusion.6 = bf16[2,14336,256]{2,1,0:T(8,128)(2,1)} fusion(bf16[2,14336,256]{2,1,0:T(8,128)(2,1)} %constant_dynamic-update-slice_fusion.7, bf16[2,1792,256]{2,1,0:T(8,128)(2,1)} %collective-permute-done.1), kind=kLoop, calls=%fused_computation.22 | loop fusion | bytes 3670016
  238.9 0.0 copy-done.2
  238.9 1.3 constant_dynamic-update-slice_fusion.5
  240.2 1.4 constant_dynamic-update-slice_fusion.4
  241.6 2.8 %constant_dynamic-update-slice_fusion.3 = bf16[2,14336,256]{2,1,0:T(8,128)(2,1)} fusion(bf16[2,14336,256]{2,1,0:T(8,128)(2,1)} %constant_dynamic-update-slice_fusion.4, bf16[2,1792,256]{2,1,0:T(8,128)(2,1)} %collective-permute-done.2), kind=kLoop, calls=%fused_computation.19 | loop fusion | bytes 3670016
  244.4 2.9 %constant_dynamic-update-slice_fusion.2 = bf16[2,14336,256]{2,1,0:T(8,128)(2,1)} fusion(bf16[2,14336,256]{2,1,0:T(8,128)(2,1)} %constant_dynamic-update-slice_fusion.3, bf16[2,1792,256]{2,1,0:T(8,128)(2,1)} %collective-permute-done.1), kind=kLoop, calls=%fused_computation.18 | loop fusion | bytes 3670016
  247.3 1.4 constant_dynamic-update-slice_fusion.1
  248.7 1.4 constant_dynamic-update-slice_fusion
  250.1 0.0 copy-start.6
  250.1 5.0 %constant_dynamic-slice_fusion = bf16[2,7168,256]{2,1,0:T(8,128)(2,1)S(1)} fusion(bf16[2,14336,256]{2,1,0:T(8,128)(2,1)} %constant_dynamic-update-slice_fusion, s32[]{:T(128)S(6)} %select_n.23), kind=kLoop, calls=%fused_computation.27 | loop fusion | bytes 14680068 | tf_op jit(solution)/shard_map/jit(_roll_dynamic)/dynamic_slice | solution.py:40
  255.0 0.0 copy-done.6
  255.1 0.0 copy-start
  255.1 1.2 fusion.1
  256.2 1.9 copy-done
  258.1 0.7 fusion.7
  (3 shorter events, 0.0 us)
Async XLA Ops:
  7.2 72.0 %reduce-scatter.2.cloned.1.call-start = ((), (), s32[]{:S(2)}) async-start(), calls=%async_computation.3 | async-start | bytes 9175040 | tf_op jit(solution)/shard_map/reduce_scatter | solution.py:15
  154.1 2.0 copy-start.5
  154.5 2.9 %copy-start.3 = (f32[2,1792,256]{2,1,0:T(8,128)S(1)}, f32[2,1792,256]{2,1,0:T(8,128)}, u32[]{:S(2)}) copy-start(f32[2,1792,256]{2,1,0:T(8,128)} %param.7) | copy-start | bytes 11010052
  154.5 3.9 %copy-start.4 = (f32[2,1792,256]{2,1,0:T(8,128)S(1)}, f32[2,1792,256]{2,1,0:T(8,128)}, u32[]{:S(2)}) copy-start(f32[2,1792,256]{2,1,0:T(8,128)} %param.8) | copy-start | bytes 11010052
  158.4 51.7 %copy-start.7 = (s32[128]{0:T(128)S(1)}, s32[128]{0:T(128)}, u32[]{:S(2)}) copy-start(s32[128]{0:T(128)} %param.11) | copy-start | bytes 1540
  163.5 22.7 %collective-permute-start = (bf16[2,1792,256]{2,1,0:T(8,128)(2,1)S(1)}, bf16[2,1792,256]{2,1,0:T(8,128)(2,1)S(1)}, u32[]{:S(2)}, u32[]{:S(2)}) collective-permute-start(bf16[2,1792,256]{2,1,0:T(8,128)(2,1)S(1)} %get-tuple-element.5), channel_id=1, source_target_pairs={{0,8},{8,16},{16,24},{24,0},{1,9},{9,17},{17,25},{25,1},{2,10},{10... | collective-permute-start | bytes 5505032 | tf_op jit(solution)/shard_map/ppermute | solution.py:37
  186.1 1.2 copy-start.1
  187.4 22.8 %collective-permute-start.1 = (bf16[2,1792,256]{2,1,0:T(8,128)(2,1)S(1)}, bf16[2,1792,256]{2,1,0:T(8,128)(2,1)}, u32[]{:S(2)}, u32[]{:S(2)}) collective-permute-start(bf16[2,1792,256]{2,1,0:T(8,128)(2,1)S(1)} %collective-permute-done), channel_id=1, source_target_pairs={{0,8},{8,16},{16,24},{24,0},{1,9},{9,17},{17,25},{25,1},{2,10},{10... | collective-permute-start | bytes 5505032 | tf_op jit(solution)/shard_map/ppermute | solution.py:37
  210.1 23.0 %collective-permute-start.2 = (bf16[2,1792,256]{2,1,0:T(8,128)(2,1)}, bf16[2,1792,256]{2,1,0:T(8,128)(2,1)}, u32[]{:S(2)}, u32[]{:S(2)}) collective-permute-start(bf16[2,1792,256]{2,1,0:T(8,128)(2,1)} %collective-permute-done.1), channel_id=1, source_target_pairs={{0,8},{8,16},{16,24},{24,0},{1,9},{9,17},{17,25},{25,1},{2,10},{10... | collective-permute-start | bytes 5505032 | tf_op jit(solution)/shard_map/ppermute | solution.py:37
  217.3 21.6 %copy-start.2 = (bf16[2,1792,256]{2,1,0:T(8,128)(2,1)S(1)}, bf16[2,1792,256]{2,1,0:T(8,128)(2,1)}, u32[]{:S(2)}) copy-start(bf16[2,1792,256]{2,1,0:T(8,128)(2,1)} %copy-done.1) | copy-start | bytes 5505028
  250.1 5.0 %copy-start.6 = (bf16[128,7168]{1,0:T(8,128)(2,1)S(1)}, bf16[128,7168]{1,0:T(8,128)(2,1)}, u32[]{:S(2)}) copy-start(bf16[128,7168]{1,0:T(8,128)(2,1)} %gather_fusion) | copy-start | bytes 5505028
  255.1 3.1 %copy-start = (bf16[2,7168,256]{2,1,0:T(8,128)(2,1)}, bf16[2,7168,256]{2,1,0:T(8,128)(2,1)S(1)}, u32[]{:S(2)}) copy-start(bf16[2,7168,256]{2,1,0:T(8,128)(2,1)S(1)} %constant_dynamic-slice_fusion) | copy-start | bytes 22020100
Sparse Core Ops, SparseCore 0:
  10.5 68.6 reduce-scatter.1
